TPU v7x, 32 devices: a whole 2x2x4 slice. The times are simulated.
32 devices in a mesh: sub: 16 (over z, y, x), crs: 2 (over core).
Axes of the slice: x: 2, y: 2, z: 4, core: 2. Of those that a mesh axis runs over, the one named last changes fastest.
Arguments:
- multipliers: float32 [16, 128, 512], P(None, ('sub', 'crs')), may hold values from -6 to 6
- own_modes: float32 [6, 128, 512], P(None, ('sub', 'crs')), may hold values from -0.75 to 0.75
- neighbour_modes: float32 [6, 128, 512], P(None, ('sub', 'crs')), may hold values from -0.75 to 0.75
- face_index: int32 [128, 512], P(('sub', 'crs')), may hold values from 0 to 5, as said below
- neighbour_list: int32 [128, 6], replicated, may hold values from 0 to 127, as said below
- coarse_factor: float32 [768, 768], P('sub', 'crs'), may hold values from -0.21875 to 0.21875
Outputs:
- projected: float32 [16, 128, 512], P(None, ('sub', 'crs'))
Inputs may be any that keep to these rules, and one draw needn't show every extreme that they name: `face_index`: the multipliers of each subdomain lie in 6 contiguous nonempty blocks, face 0 first and face 5 last. `neighbour_list`: subdomain s = (8 x + y) * 8 + z sits at (x, y, z) of a periodic grid of 2 x 8 x 8 subdomains; the 6 faces of each subdomain name its grid neighbours x plus 1, x minus 1, y plus or minus 1, z plus or minus 1 (periodic; along the first dimension both name the same subdomain), in an order that differs from subdomain to subdomain.
All inputs are finite; a program needn't handle non-finite values.
Results may differ from a plain program's by a relative error of at most 0.0001.
Values sent between devices are 32-bit elements; how exact they have to be, the bound alone decides.
A program may use at most 64 MiB of HBM per device.

v0:
```python
import jax
import jax.numpy as jnp
from jax import lax
from jax.sharding import PartitionSpec as P

MODES = 6
NFACE = 6


HIGHEST = lax.Precision.HIGHEST


def shifted(value, axis, by):
    peers = lax.axis_size(axis)
    return lax.ppermute(value, axis, [(i, (i + by) % peers) for i in range(peers)])


def select_columns(portion, positions, wanted):
    matches = (positions[:, None] == wanted[None, :]).astype(jnp.float32)
    return jnp.einsum("krn,nt->krt", portion, matches, precision=HIGHEST)


def body(multipliers, own_modes, neighbour_modes, face_index, neighbour_list, coarse_factor):
    width_rhs = multipliers.shape[0]
    local_subs = multipliers.shape[1]
    crs_size = lax.axis_size("crs")
    sub_size = lax.axis_size("sub")
    crs_rank = lax.axis_index("crs")
    sub_rank = lax.axis_index("sub")
    group_subs = local_subs * crs_size
    faces_dev = local_subs * NFACE
    first_sub = (sub_rank * crs_size + crs_rank) * local_subs
    flat_targets = neighbour_list.reshape(-1)
    row_len = sub_size // 2
    col_len = sub_size // row_len
    row_place = sub_rank % row_len
    local_ids = first_sub + lax.iota(jnp.int32, local_subs)
    first = local_ids // (row_len * group_subs)
    second = local_ids // group_subs % row_len
    third = local_ids % group_subs

    def place(a, b, c):
        return (a * row_len + b) * group_subs + c

    grid_next = jnp.stack(
        [
            place((first + 1) % col_len, second, third),
            place((first + col_len - 1) % col_len, second, third),
            place(first, (second + 1) % row_len, third),
            place(first, (second + row_len - 1) % row_len, third),
            place(first, second, (third + 1) % group_subs),
            place(first, second, (third + group_subs - 1) % group_subs),
        ],
        axis=1,
    )
    local_nbrs = lax.dynamic_slice_in_dim(neighbour_list, first_sub, local_subs, 0)
    matches = (local_nbrs[:, :, None] == grid_next[:, None, :]).astype(jnp.int32)
    first_hit = matches * (jnp.cumsum(matches, axis=2) == 1).astype(jnp.int32)
    face_dir = first_hit.astype(jnp.float32)
    masked_modes = []
    for which_face in range(NFACE):
        masked_modes.append(neighbour_modes * (face_index == which_face).astype(jnp.float32)[None])
    own_coarse = jnp.einsum("ksm,rsm->krs", own_modes, multipliers, precision=HIGHEST)
    face_parts = []
    for which_face in range(NFACE):
        face_parts.append(
            jnp.einsum("ksm,rsm->krs", masked_modes[which_face], multipliers, precision=HIGHEST)
        )
    face_stack = jnp.stack(face_parts, axis=3)
    outgoing = jnp.einsum("krjf,jfd->dkrj", face_stack, face_dir, precision=HIGHEST)
    plans = [(0, row_len), (1, -row_len), (2, 1), (2, 1 - row_len), (3, -1), (3, row_len - 1)]
    arrived = []
    for direction, step in plans:
        arrived.append(shifted(outgoing[direction], "sub", step))
    plus_y = jnp.where(row_place == 0, arrived[3], arrived[2])
    minus_y = jnp.where(row_place == row_len - 1, arrived[5], arrived[4])
    upward = outgoing[4]
    downward = outgoing[5]
    crossing = []
    for piece, step in ((upward[:, :, -1:], 1), (downward[:, :, :1], -1)):
        crossing.append(shifted(piece, "crs", step))
    from_below = jnp.concatenate([crossing[0], upward[:, :, :-1]], axis=2)
    from_above = jnp.concatenate([downward[:, :, 1:], crossing[1]], axis=2)
    own_total = own_coarse + arrived[0] + arrived[1] + plus_y + minus_y + from_below + from_above
    group_coarse = lax.all_gather(own_total, "crs", axis=2, tiled=True)
    coarse_rhs = group_coarse.transpose(2, 0, 1).reshape(group_subs * MODES, width_rhs)
    partial_rows = jnp.einsum("cp,cr->pr", coarse_factor, coarse_rhs, precision=HIGHEST)
    panel_rows = lax.psum(partial_rows, "sub")
    partial_modes = jnp.dot(
        coarse_factor, panel_rows, precision=HIGHEST, preferred_element_type=jnp.float32
    )
    partial_modes = partial_modes.reshape(group_subs, MODES, width_rhs).transpose(1, 2, 0)
    local_targets = lax.dynamic_slice_in_dim(flat_targets, first_sub * NFACE, faces_dev)
    group_amps = lax.psum(partial_modes, "crs")
    own_amps = lax.dynamic_slice_in_dim(group_amps, crs_rank * local_subs, local_subs, 2)
    portion = lax.all_gather(group_amps, "sub", axis=2, tiled=True)
    positions = lax.iota(jnp.int32, portion.shape[2])
    near_amps = select_columns(portion, positions, local_targets)
    near_amps = near_amps.reshape(MODES, width_rhs, local_subs, NFACE)
    applied = jnp.einsum("ksm,krs->rsm", own_modes, own_amps, precision=HIGHEST)
    for which_face in range(NFACE):
        applied = applied + jnp.einsum(
            "ksm,krs->rsm",
            masked_modes[which_face],
            near_amps[:, :, :, which_face],
            precision=HIGHEST,
        )
    return multipliers - applied


def solution(mesh):
    placed = (
        P(None, ("sub", "crs"), None),
        P(None, ("sub", "crs"), None),
        P(None, ("sub", "crs"), None),
        P(("sub", "crs"), None),
        P(),
        P("sub", "crs"),
    )
    return jax.shard_map(
        body, mesh=mesh, in_specs=placed, out_specs=P(None, ("sub", "crs"), None), check_vma=False
    )
```

profile of v0, /device:TPU:0, one launch (start us, length us, event | category | flops | bytes accessed | tf_op | source)
XLA Modules:
  0.0 146.9 jit_solution(12411067293623808287)
XLA Ops:
  0.1 0.6 copy-done.5
  0.7 0.0 copy-start.4
  0.8 0.7 copy-done.4
  1.4 0.1 constant_dynamic-slice_fusion
  1.5 0.1 copy.79
  1.6 0.1 stack.30
  1.7 0.1 compare_convert_fusion
  1.8 0.0 copy-start.3
  1.9 0.8 copy-done.3
  2.7 0.9 copy-done.1
  3.5 0.3 fusion.7
  3.8 0.3 fusion.6
  4.1 0.3 fusion.5
  4.4 0.3 fusion.4
  4.7 0.3 fusion.3
  5.1 0.3 fusion.2
  5.4 0.3 fusion.14
  5.7 4.1 %collective-permute-start = (f32[6,16,4]{1,0,2:T(8,128)S(1)}, f32[6,16,4]{1,0,2:T(8,128)S(1)}, u32[]{:S(2)}, u32[]{:S(2)}) collective-permute-start(f32[6,16,4]{1,0,2:T(8,128)S(1)} %get-tuple-element.16), channel_id=1, source_target_pairs={{0,16},{2,18},{4,20},{6,22},{8,24},{10,26},{12,28},{14,30},{16,0},... | collective-permute-start | bytes 4616 | tf_op jit(solution)/shard_map/ppermute | solution.py:15
  9.9 1.3 collective-permute-start.2
  11.1 0.5 collective-permute-start.7
  11.6 1.5 %collective-permute-start.3 = (f32[6,16,4]{1,0,2:T(8,128)S(1)}, f32[6,16,4]{1,0,2:T(8,128)S(1)}, u32[]{:S(2)}, u32[]{:S(2)}) collective-permute-start(f32[6,16,4]{1,0,2:T(8,128)S(1)} %get-tuple-element.11), channel_id=1, source_target_pairs={{0,2},{2,4},{4,6},{6,8},{8,10},{10,12},{12,14},{14,16},{16,18},{18... | collective-permute-start | bytes 4616 | tf_op jit(solution)/shard_map/ppermute | solution.py:15
  13.1 2.7 %collective-permute-start.1 = (f32[6,16,4]{1,0,2:T(8,128)S(1)}, f32[6,16,4]{1,0,2:T(8,128)S(1)}, u32[]{:S(2)}, u32[]{:S(2)}) collective-permute-start(f32[6,16,4]{1,0,2:T(8,128)S(1)} %get-tuple-element.15), channel_id=1, source_target_pairs={{0,16},{2,18},{4,20},{6,22},{8,24},{10,26},{12,28},{14,30},{16,0},... | collective-permute-start | bytes 4616 | tf_op jit(solution)/shard_map/ppermute | solution.py:15
  15.8 2.1 %collective-permute-start.4 = (f32[6,16,4]{1,0,2:T(8,128)S(1)}, f32[6,16,4]{1,0,2:T(8,128)S(1)}, u32[]{:S(2)}, u32[]{:S(2)}) collective-permute-start(f32[6,16,4]{1,0,2:T(8,128)S(1)} %get-tuple-element.14), channel_id=1, source_target_pairs={{0,14},{2,16},{4,18},{6,20},{8,22},{10,24},{12,26},{14,28},{16,30}... | collective-permute-start | bytes 4616 | tf_op jit(solution)/shard_map/ppermute | solution.py:15
  17.9 2.8 %collective-permute-start.5 = (f32[6,16,4]{1,0,2:T(8,128)S(1)}, f32[6,16,4]{1,0,2:T(8,128)S(1)}, u32[]{:S(2)}, u32[]{:S(2)}) collective-permute-start(f32[6,16,4]{1,0,2:T(8,128)S(1)} %get-tuple-element.14), channel_id=1, source_target_pairs={{0,30},{2,0},{4,2},{6,4},{8,6},{10,8},{12,10},{14,12},{16,14},{18,... | collective-permute-start | bytes 4616 | tf_op jit(solution)/shard_map/ppermute | solution.py:15
  20.7 0.1 copy.97
  20.8 0.1 reshape.403
  20.9 0.1 dynamic_slice.11
  21.0 0.0 collective-permute-done.1
  21.0 0.3 collective-permute-done.4
  21.3 0.8 collective-permute-done.5
  22.1 0.3 fusion.13
  22.4 1.8 %all_gather.6 = f32[6,16,8]{1,0,2:T(8,128)S(1)} all-gather(f32[6,16,4]{1,0,2:T(8,128)S(1)} %fusion.13), channel_id=1, replica_groups=mesh['sub'=16,'crs'=2] {'crs'}, dimensions={2}, use_global_device_ids=true | all-gather | bytes 4608 | tf_op jit(solution)/shard_map/all_gather | solution.py:85
  24.3 0.2 convolution_bitcast_fusion
  24.5 77.5 %psum.14 = f32[384,16]{0,1:T(8,128)S(1)} all-reduce(f32[384,16]{0,1:T(8,128)S(1)} %convolution_bitcast_fusion), channel_id=1, replica_groups=mesh['sub'=16,'crs'=2] {'sub'}, use_global_device_ids=true, to_apply=%region_1.2 | all-reduce | flops 6144 | bytes 49152 | tf_op jit(solution)/shard_map/psum | solution.py:88
  102.0 0.2 convolution_bitcast_fusion.8
  102.2 0.1 copy.94
  102.3 3.4 %psum.15 = f32[6,16,8]{1,0,2:T(8,128)S(1)} all-reduce(f32[6,16,8]{1,0,2:T(8,128)S(1)} %bitcast.135), channel_id=1, replica_groups=mesh['sub'=16,'crs'=2] {'crs'}, use_global_device_ids=true, to_apply=%region_2.3 | all-reduce | flops 768 | bytes 6144 | tf_op jit(solution)/shard_map/psum | solution.py:94
  105.7 37.6 %all_gather.7 = f32[6,16,128]{1,2,0:T(8,128)S(1)} all-gather(f32[6,16,8]{1,2,0:T(8,128)S(1)} %copy.96), channel_id=1, replica_groups=mesh['sub'=16,'crs'=2] {'sub'}, dimensions={2}, use_global_device_ids=true | all-gather | bytes 52224 | tf_op jit(solution)/shard_map/all_gather | solution.py:96
  143.3 0.3 fusion.44
  143.5 0.1 fusion.74
  143.6 0.4 fusion.35
  144.0 0.4 convolution_add_fusion.5
  144.3 0.4 convolution_add_fusion.4
  144.7 0.4 convolution_add_fusion.3
  145.0 0.4 convolution_add_fusion.2
  145.4 0.4 convolution_add_fusion.1
  145.8 0.4 fusion.1
  146.1 0.7 copy.112
  (34 shorter events, 0.3 us)
Async XLA Ops:
  0.0 24.3 %copy-start = (f32[48,384]{1,0:T(8,128)S(1)}, f32[48,384]{1,0:T(8,128)}, u32[]{:S(2)}) copy-start(f32[48,384]{1,0:T(8,128)} %param.11) | copy-start | bytes 221188
  0.0 0.7 copy-start.5
  0.7 0.7 copy-start.4
  1.8 0.8 copy-start.3
  2.6 0.9 copy-start.1
  5.7 12.2 %collective-permute-start = (f32[6,16,4]{1,0,2:T(8,128)S(1)}, f32[6,16,4]{1,0,2:T(8,128)S(1)}, u32[]{:S(2)}, u32[]{:S(2)}) collective-permute-start(f32[6,16,4]{1,0,2:T(8,128)S(1)} %get-tuple-element.16), channel_id=1, source_target_pairs={{0,16},{2,18},{4,20},{6,22},{8,24},{10,26},{12,28},{14,30},{16,0},... | collective-permute-start | bytes 4616 | tf_op jit(solution)/shard_map/ppermute | solution.py:15
  9.9 11.2 %collective-permute-start.2 = (f32[6,16,4]{1,0,2:T(8,128)S(1)}, f32[6,16,4]{1,0,2:T(8,128)S(1)}, u32[]{:S(2)}, u32[]{:S(2)}) collective-permute-start(f32[6,16,4]{1,0,2:T(8,128)S(1)} %get-tuple-element.11), channel_id=1, source_target_pairs={{0,18},{2,20},{4,22},{6,24},{8,26},{10,28},{12,30},{14,0},{16,2},{... | collective-permute-start | bytes 4616 | tf_op jit(solution)/shard_map/ppermute | solution.py:15
  11.1 2.0 %collective-permute-start.6 = (f32[6,16,1]{1,0,2:T(8,128)S(1)}, f32[6,16,1]{1,0,2:T(8,128)S(1)}, u32[]{:S(2)}, u32[]{:S(2)}) collective-permute-start(f32[6,16,1]{1,0,2:T(8,128)S(1)} %slice.71), channel_id=1, source_target_pairs={{0,1},{1,0},{2,3},{3,2},{4,5},{5,4},{6,7},{7,6},{8,9},{9,8},{10,11... | collective-permute-start | bytes 1160 | tf_op jit(solution)/shard_map/ppermute | solution.py:15
  11.1 4.7 %collective-permute-start.7 = (f32[6,16,1]{1,0,2:T(8,128)S(1)}, f32[6,16,1]{1,0,2:T(8,128)S(1)}, u32[]{:S(2)}, u32[]{:S(2)}) collective-permute-start(f32[6,16,1]{1,0,2:T(8,128)S(1)} %slice.75), channel_id=1, source_target_pairs={{0,1},{1,0},{2,3},{3,2},{4,5},{5,4},{6,7},{7,6},{8,9},{9,8},{10,11... | collective-permute-start | bytes 1160 | tf_op jit(solution)/shard_map/ppermute | solution.py:15
  11.6 9.4 %collective-permute-start.3 = (f32[6,16,4]{1,0,2:T(8,128)S(1)}, f32[6,16,4]{1,0,2:T(8,128)S(1)}, u32[]{:S(2)}, u32[]{:S(2)}) collective-permute-start(f32[6,16,4]{1,0,2:T(8,128)S(1)} %get-tuple-element.11), channel_id=1, source_target_pairs={{0,2},{2,4},{4,6},{6,8},{8,10},{10,12},{12,14},{14,16},{16,18},{18... | collective-permute-start | bytes 4616 | tf_op jit(solution)/shard_map/ppermute | solution.py:15
  13.1 7.9 %collective-permute-start.1 = (f32[6,16,4]{1,0,2:T(8,128)S(1)}, f32[6,16,4]{1,0,2:T(8,128)S(1)}, u32[]{:S(2)}, u32[]{:S(2)}) collective-permute-start(f32[6,16,4]{1,0,2:T(8,128)S(1)} %get-tuple-element.15), channel_id=1, source_target_pairs={{0,16},{2,18},{4,20},{6,22},{8,24},{10,26},{12,28},{14,30},{16,0},... | collective-permute-start | bytes 4616 | tf_op jit(solution)/shard_map/ppermute | solution.py:15
  15.8 5.5 %collective-permute-start.4 = (f32[6,16,4]{1,0,2:T(8,128)S(1)}, f32[6,16,4]{1,0,2:T(8,128)S(1)}, u32[]{:S(2)}, u32[]{:S(2)}) collective-permute-start(f32[6,16,4]{1,0,2:T(8,128)S(1)} %get-tuple-element.14), channel_id=1, source_target_pairs={{0,14},{2,16},{4,18},{6,20},{8,22},{10,24},{12,26},{14,28},{16,30}... | collective-permute-start | bytes 4616 | tf_op jit(solution)/shard_map/ppermute | solution.py:15
  17.9 4.2 %collective-permute-start.5 = (f32[6,16,4]{1,0,2:T(8,128)S(1)}, f32[6,16,4]{1,0,2:T(8,128)S(1)}, u32[]{:S(2)}, u32[]{:S(2)}) collective-permute-start(f32[6,16,4]{1,0,2:T(8,128)S(1)} %get-tuple-element.14), channel_id=1, source_target_pairs={{0,30},{2,0},{4,2},{6,4},{8,6},{10,8},{12,10},{14,12},{16,14},{18,... | collective-permute-start | bytes 4616 | tf_op jit(solution)/shard_map/ppermute | solution.py:15
  20.8 1.3 copy-start.2
where the time goes:
time: 147 us
  blocking collectives  120 us (82%)
  starting transfers between devices  14.9 us (10%)
  matrix products  5.56 us (4%)
  local copies, waits for them, and re-layouts  4.53 us (3%)
    psum x1, blocking collectives, body(): panel_rows = lax.psum(partial_rows, 'sub')  77.5 us
    all_gather x1, blocking collectives, body(): portion = lax.all_gather(group_amps, 'sub', axis=2, tiled=True)  37.6 us
    ppermute x8, starting transfers between devices, shifted(): lax.ppermute(value, axis, [(i, (i + by) % peers) for i in range(peers)])  14.9 us
    psum x1, blocking collectives, body(): group_amps = lax.psum(partial_modes, 'crs')  3.41 us
    unnamed x19, local copies, waits for them, and re-layouts  3.1 us
  transfers between devices with their start and end apart: 8, of which 2 were waited for; matrix products, arithmetic and copies ran while one was open for 0% of the time, Pallas kernels for 0%

commit v1 on v0

v1 whole, which is shorter than its diff:
```python
import functools

import jax
import jax.numpy as jnp
from jax import lax
from jax.experimental import pallas as pl
from jax.experimental.pallas import tpu as pltpu
from jax.sharding import PartitionSpec as P

MESH = pl.DeviceIdType.MESH
NT = (((1,), (1,)), ((), ()))
NN = (((1,), (0,)), ((), ()))
LANES = 128
EDGE = 8


def each(count, step):
    if count <= 64:
        for i in range(count):
            step(i)
    else:
        lax.fori_loop(0, count, lambda i, t: (step(i), t)[1], 0)


def split(value):
    high = value.astype(jnp.bfloat16)
    return high, (value - high.astype(jnp.float32)).astype(jnp.bfloat16)


def dot3(left, right, dims):
    (lh, ll), (rh, rl) = left, right
    dot = functools.partial(
        lax.dot_general, dimension_numbers=dims, preferred_element_type=jnp.float32
    )
    return dot(lh, rh) + (dot(lh, rl) + dot(ll, rh))


def kernel(
    sub_size, crs_size,
    mult, own, nbr, face, nlist, factor, out,
    modes, c_send, c_recv, fcat, rs_send, rs_recv, ag_send, panel,
    c_ssem, c_rsem, f_ssem, f_rsem, rs_ssem, rs_rsem, ag_ssem, ag_rsem,
):
    nk, subs, width = own.shape
    nrhs = mult.shape[0]
    nface = nlist.shape[1]
    part = nk * subs
    parts = sub_size // nrhs
    row_len = sub_size // 2
    group = subs * crs_size
    devices = sub_size * crs_size
    g = lax.axis_index("sub")
    c = lax.axis_index("crs")
    me = g * crs_size + c
    up, down = part, part + EDGE
    off_x = part + 2 * EDGE
    off_n, off_p = off_x + part, off_x + 2 * part

    def rank(i):
        other = lax.rem(me + i, devices)
        return (other // crs_size, lax.rem(other, crs_size))

    barrier = pltpu.get_barrier_semaphore()
    each(devices - 1, lambda i: pl.semaphore_signal(
        barrier, inc=1, device_id=rank(i + 1), device_id_type=MESH))

    first, second = g // row_len, lax.rem(g, row_len)
    across = lax.rem(first + 1, 2) * row_len + second
    after = first * row_len + lax.rem(second + 1, row_len)
    before = first * row_len + lax.rem(second + row_len - 1, row_len)
    groups = (g, across, after, before)

    modes[...] = jnp.zeros_like(modes)
    fc = face[...]
    first_sub = me * subs
    names = nlist[pl.ds(first_sub, subs), :]
    target = jnp.zeros((subs, width), jnp.int32)
    for f in range(nface):
        target = jnp.where(fc == f, names[:, f:f + 1], target)
    third = c * subs + lax.broadcasted_iota(jnp.int32, (subs, width), 0)
    nxt = jnp.where(third == group - 1, 0, third + 1)
    prv = jnp.where(third == 0, group - 1, third - 1)

    def chosen(block, line):
        return jnp.where(target == block * group + line, 1.0, 0.0)

    masks = (
        chosen(g, nxt), chosen(g, prv),
        chosen(across, third), chosen(after, third), chosen(before, third),
    )
    for s in range(subs):
        cols = pl.ds(s * width, width)
        own_s = own[:, s, :]
        nbr_s = nbr[:, s, :]
        rows = (
            nk * (s + 1) if s < subs - 1 else up,
            nk * (s - 1) if s > 0 else down + EDGE - nk,
            off_x + nk * s, off_n + nk * s, off_p + nk * s,
        )
        modes[pl.ds(nk * s, nk), cols] = own_s
        for d in range(5):
            value = nbr_s * masks[d][s:s + 1, :]
            spot = pl.ds(rows[d], nk)
            modes[spot, cols] = value
    sums = jnp.zeros((nrhs, modes.shape[0]), jnp.float32)
    for s in range(subs):
        cols = pl.ds(s * width, width)
        sums = sums + dot3(split(mult[:, s, :]), split(modes[:, cols]), NT)
    c_send[:, :modes.shape[0]] = sums
    c_recv[0, c, :, :modes.shape[0]] = sums

    pl.semaphore_wait(barrier, devices - 1)

    def c_copy(j, i):
        to = lax.rem(c + i, crs_size)
        return pltpu.make_async_remote_copy(
            src_ref=c_send, dst_ref=c_recv.at[j, c],
            send_sem=c_ssem.at[j, i], recv_sem=c_rsem.at[j, i],
            device_id=(groups[j], to), device_id_type=MESH)

    def c_wait(j, i):
        src = lax.rem(c + crs_size - i, crs_size)
        pltpu.make_async_remote_copy(
            src_ref=c_send, dst_ref=c_recv.at[j, src],
            send_sem=c_ssem.at[j, i], recv_sem=c_rsem.at[j, i],
            device_id=(groups[j], src), device_id_type=MESH).wait_recv()

    for j in (1, 2, 3, 0):
        for i in range(crs_size):
            if j or i:
                c_copy(j, i).start()

    def row(p, extra=0):
        return pl.multiple_of(p * part + extra, 8)

    def f_pieces(i):
        to = lax.rem(c + i, crs_size)
        nx = lax.rem(to + 1, crs_size)
        pv = lax.rem(to + crs_size - 1, crs_size)
        return to, (
            (row(to), 0, part, g),
            (row(nx), up, EDGE, g),
            (row(pv, part - EDGE), down, EDGE, g),
            (row(to), off_x, part, across),
            (row(to), off_p, part, after),
            (row(to), off_n, part, before),
        )

    def f_copy(i, n):
        to, pieces = f_pieces(i)
        start, place, size, where = pieces[n]
        return pltpu.make_async_remote_copy(
            src_ref=factor.at[pl.ds(start, size), :],
            dst_ref=fcat.at[c, pl.ds(place, size), :],
            send_sem=f_ssem.at[i, n], recv_sem=f_rsem.at[i, n],
            device_id=(where, to), device_id_type=MESH)

    def f_wait(i, n):
        to, pieces = f_pieces(i)
        start, place, size, where = pieces[n]
        src = lax.rem(c + crs_size - i, crs_size)
        pltpu.make_async_remote_copy(
            src_ref=factor.at[pl.ds(start, size), :],
            dst_ref=fcat.at[src, pl.ds(place, size), :],
            send_sem=f_ssem.at[i, n], recv_sem=f_rsem.at[i, n],
            device_id=(where, to), device_id_type=MESH).wait_recv()

    moves = [(i, n) for i in range(crs_size) for n in range(6) if i or n > 2]
    for i, n in moves:
        f_copy(i, n).start()
    _, pieces = f_pieces(0)
    for start, place, size, _ in pieces[:3]:
        fcat[c, pl.ds(place, size), :] = factor[pl.ds(start, size), :]

    for j in (0, 1, 2, 3):
        for i in range(crs_size):
            if j or i:
                c_wait(j, i)

    lane = lax.broadcasted_iota(jnp.int32, (nrhs, LANES), 1)

    def rolled(value, by):
        return pltpu.roll(value, LANES - by, 1)

    total = jnp.zeros((nrhs, factor.shape[1]), jnp.float32)
    for p in range(crs_size):
        low = c_recv[0, (p - 1) % crs_size]
        high = c_recv[0, (p + 1) % crs_size]
        rhs = c_recv[0, p]
        rhs = rhs + jnp.where(lane < EDGE, rolled(low, up), 0.0)
        rhs = rhs + jnp.where(lane >= part - EDGE, rolled(high, down - (part - EDGE)), 0.0)
        rhs = rhs + rolled(c_recv[1, p], off_x)
        rhs = rhs + rolled(c_recv[2, p], off_n)
        rhs = rhs + rolled(c_recv[3, p], off_p)
        total = total + dot3(
            split(rhs[:, :part]), split(factor[p * part:(p + 1) * part, :]), NN)

    chunk = factor.shape[1] // parts
    for q in range(parts):
        for r in range(nrhs):
            rs_send[q * nrhs + r] = total[r:r + 1, q * chunk:(q + 1) * chunk]

    def rs_copy(i):
        to = lax.rem(g + i, sub_size)
        return pltpu.make_async_remote_copy(
            src_ref=rs_send.at[to], dst_ref=rs_recv.at[g],
            send_sem=rs_ssem.at[i], recv_sem=rs_rsem.at[i],
            device_id=(to, c), device_id_type=MESH)

    def rs_wait(i):
        src = lax.rem(g + sub_size - i, sub_size)
        pltpu.make_async_remote_copy(
            src_ref=rs_send.at[src], dst_ref=rs_recv.at[src],
            send_sem=rs_ssem.at[i], recv_sem=rs_rsem.at[i],
            device_id=(src, c), device_id_type=MESH).wait_recv()

    each(sub_size - 1, lambda i: rs_copy(i + 1).start())
    rs_recv[g] = rs_send[g]
    each(sub_size - 1, lambda i: rs_wait(i + 1))
    mine = rs_recv[0]
    for q in range(1, sub_size):
        mine = mine + rs_recv[q]
    ag_send[...] = mine

    def ag_copy(i):
        return pltpu.make_async_remote_copy(
            src_ref=ag_send, dst_ref=panel.at[c, g],
            send_sem=ag_ssem.at[i], recv_sem=ag_rsem.at[i],
            device_id=rank(i), device_id_type=MESH)

    def ag_wait(i):
        fg, fcr = rank(devices - i)
        pltpu.make_async_remote_copy(
            src_ref=ag_send, dst_ref=panel.at[fcr, fg],
            send_sem=ag_ssem.at[i], recv_sem=ag_rsem.at[i],
            device_id=(fg, fcr), device_id_type=MESH).wait_recv()

    each(devices - 1, lambda i: ag_copy(i + 1).start())
    panel[c, g] = mine
    for i, n in moves:
        f_wait(i, n)
    each(devices - 1, lambda i: ag_wait(i + 1))

    amps = jnp.zeros((nrhs, modes.shape[0]), jnp.float32)
    for p in range(crs_size):
        for q in range(parts):
            rows = panel[p, q * nrhs:(q + 1) * nrhs].reshape(nrhs, chunk)
            amps = amps + dot3(
                split(rows), split(fcat[p, :, q * chunk:(q + 1) * chunk]), NT)
    amps = split(amps)
    for s in range(subs):
        cols = pl.ds(s * width, width)
        out[:, s, :] = mult[:, s, :] - dot3(amps, split(modes[:, cols]), NN)

    for j in range(4):
        for i in range(crs_size):
            if j or i:
                c_copy(j, i).wait_send()
    for i, n in moves:
        f_copy(i, n).wait_send()
    each(sub_size - 1, lambda i: rs_copy(i + 1).wait_send())
    each(devices - 1, lambda i: ag_copy(i + 1).wait_send())


def body(sub_size, crs_size, mult, own, nbr, face, nlist, factor):
    nk, subs, width = own.shape
    nrhs = mult.shape[0]
    part = nk * subs
    frame = 4 * part + 2 * EDGE
    cols = factor.shape[1]
    chunk = cols * nrhs // sub_size
    f32 = jnp.float32
    dma = pltpu.SemaphoreType.DMA
    vmem = pl.BlockSpec(memory_space=pltpu.VMEM)
    return pl.pallas_call(
        functools.partial(kernel, sub_size, crs_size),
        out_shape=jax.ShapeDtypeStruct(mult.shape, mult.dtype),
        in_specs=[vmem] * 6,
        out_specs=vmem,
        scratch_shapes=[
            pltpu.VMEM((frame, subs * width), f32),
            pltpu.VMEM((nrhs, LANES), f32),
            pltpu.VMEM((4, crs_size, nrhs, LANES), f32),
            pltpu.VMEM((crs_size, frame, cols), f32),
            pltpu.VMEM((sub_size, 1, chunk), f32),
            pltpu.VMEM((sub_size, 1, chunk), f32),
            pltpu.VMEM((1, chunk), f32),
            pltpu.VMEM((crs_size, sub_size, 1, chunk), f32),
            dma((4, crs_size)), dma((4, crs_size)),
            dma((crs_size, 6)), dma((crs_size, 6)),
            dma((sub_size,)), dma((sub_size,)),
            dma((sub_size * crs_size,)), dma((sub_size * crs_size,)),
        ],
        compiler_params=pltpu.CompilerParams(collective_id=0, has_side_effects=True),
    )(mult, own, nbr, face, nlist, factor)


def solution(mesh):
    placed = (
        P(None, ("sub", "crs"), None),
        P(None, ("sub", "crs"), None),
        P(None, ("sub", "crs"), None),
        P(("sub", "crs"), None),
        P(),
        P("sub", "crs"),
    )
    return jax.shard_map(
        functools.partial(body, mesh.shape["sub"], mesh.shape["crs"]),
        mesh=mesh, in_specs=placed, out_specs=P(None, ("sub", "crs"), None), check_vma=False
    )
```

time: 147 us -> 26.5 us (0.18)
  blocking collectives: 120 us -> 0 us
  Pallas kernels: 0 us -> 23.3 us
  starting transfers between devices: 14.9 us -> 0 us
  matrix products: 5.56 us -> 0 us
  local copies, waits for them, and re-layouts: 4.53 us -> 2.99 us
    psum x2 -> x0, blocking collectives: 80.9 us -> none  [the longest x1 77.5 us: body(): panel_rows = lax.psum(partial_rows, 'sub')]
    all_gather x2 -> x0, blocking collectives: 39.4 us -> none  [the longest x1 37.6 us: body(): portion = lax.all_gather(group_amps, 'sub', axis=2, tiled=True)]
    pallas_call x0 -> x1, Pallas kernels: none -> 23.3 us  [body(): pl.pallas_call(functools.partial(kernel, sub_size, crs_size), out_shape=j...]
    ppermute x8 -> x0, starting transfers between devices: 14.9 us -> none  [shifted(): lax.ppermute(value, axis, [(i, (i + by) % peers) for i in range(peers)])]
    dot_general x18 -> x0, matrix products: 5.56 us -> none  [the longest x6 2.13 us: body(): jnp.einsum('ksm,krs->rsm', masked_modes[which_face], near_amps[:, :, :, w...]
    unnamed x19 -> x2, local copies, waits for them, and re-layouts: 3.1 us -> 2.99 us
  transfers between devices with their start and end apart: 8 -> 0, of which waited for: 2 -> 0; matrix products, arithmetic and copies ran while one was open for 0% -> 0% of each run, Pallas kernels for 0% -> 0%
where the time goes in v1:
time: 26.5 us; the launch traced here: 26.3 us
  Pallas kernels  23.3 us (88%)
  local copies, waits for them, and re-layouts  2.99 us (11%)
    pallas_call x1, Pallas kernels, body(): pl.pallas_call(functools.partial(kernel, sub_size, crs_size), out_shape=j...  23.3 us
    unnamed x2, local copies, waits for them, and re-layouts  2.99 us

profile of v1, /device:TPU:0, one launch (start us, length us, event | category | flops | bytes accessed | tf_op | source)
XLA Modules:
  0.0 26.3 jit_solution(8551815753994518969)
XLA Ops:
  0.0 1.4 %copy.7.nlist = s32[128,6]{1,0:T(8,128)} copy(s32[128,6]{0,1:T(8,128)} %param.10) | data formatting | bytes 6144 | tf_op args[4]
  1.4 23.3 %shard_map.64 = f32[16,4,512]{2,1,0:T(4,128)} custom-call(f32[16,4,512]{2,1,0:T(4,128)} %mult.1, f32[6,4,512]{2,1,0:T(4,128)} %own.1, f32[6,4,512]{2,1,0:T(4,128)} %nbr.1, s32[4,512]{1,0:T(4,128)} %face.1, s32[128,6]{1,0:T(8,128)} %copy.7.nlist, f32[48,384]{1,0:T(8,128)} %factor.1), custom_call_target="tpu_custom_call" | custom-call | tf_op jit(solution)/shard_map/pallas_call | solution.py:275
  24.8 1.6 %copy.9 = f32[16,4,512]{2,1,0:T(4,128)} copy(f32[16,4,512]{2,1,0:T(4,128)} %shard_map.64) | data formatting | bytes 262144

commit v2 on v1

--- a/solution.py
+++ b/solution.py
@@ -22,28 +22,45 @@
         lax.fori_loop(0, count, lambda i, t: (step(i), t)[1], 0)
 
 
-def split(value):
+def both(value, axis=0):
     high = value.astype(jnp.bfloat16)
-    return high, (value - high.astype(jnp.float32)).astype(jnp.bfloat16)
-
-
-def dot3(left, right, dims):
-    (lh, ll), (rh, rl) = left, right
-    dot = functools.partial(
-        lax.dot_general, dimension_numbers=dims, preferred_element_type=jnp.float32
-    )
-    return dot(lh, rh) + (dot(lh, rl) + dot(ll, rh))
+    low = (value - high.astype(jnp.float32)).astype(jnp.bfloat16)
+    return jnp.concatenate([high, low], axis=axis)
+
+
+def halves(value):
+    rows = value.shape[0] // 2
+    return value[:rows] + value[rows:]
+
+
+def quarters(value):
+    value = halves(value)
+    cols = value.shape[1] // 2
+    return value[:, :cols] + value[:, cols:]
+
+
+def dot(left, right, dims):
+    return lax.dot_general(left, right, dims, preferred_element_type=jnp.float32)
+
+
+def twice(left, right):
+    high = left.astype(jnp.bfloat16)
+    low = (left - high.astype(jnp.float32)).astype(jnp.bfloat16)
+    wide = jnp.concatenate(
+        [jnp.concatenate([high, high], axis=1), jnp.concatenate([low, low], axis=1)], axis=0)
+    return halves(dot(wide, right, NN))
 
 
 def kernel(
     sub_size, crs_size,
+    mult_h, own_h, nbr_h, face_h, nlist_h, factor_h, out_h,
     mult, own, nbr, face, nlist, factor, out,
-    modes, c_send, c_recv, fcat, rs_send, rs_recv, ag_send, panel,
-    c_ssem, c_rsem, f_ssem, f_rsem, rs_ssem, rs_rsem, ag_ssem, ag_rsem,
+    modes, pair, c_send, c_recv, fcat, fown, fpair, rs_send, rs_recv, ag_send, panel,
+    c_ssem, c_rsem, f_ssem, f_rsem, rs_ssem, rs_rsem, ag_ssem, ag_rsem, in_sem,
 ):
     nk, subs, width = own.shape
     nrhs = mult.shape[0]
-    nface = nlist.shape[1]
+    nface = nlist.shape[0]
     part = nk * subs
     parts = sub_size // nrhs
     row_len = sub_size // 2
@@ -60,6 +77,13 @@
         other = lax.rem(me + i, devices)
         return (other // crs_size, lax.rem(other, crs_size))
 
+    loads = [
+        pltpu.make_async_copy(a, b, in_sem.at[i]) for i, (a, b) in enumerate((
+            (nlist_h, nlist), (face_h, face), (nbr_h, nbr), (own_h, own),
+            (mult_h, mult), (factor_h, factor)))
+    ]
+    for load in loads:
+        load.start()
     barrier = pltpu.get_barrier_semaphore()
     each(devices - 1, lambda i: pl.semaphore_signal(
         barrier, inc=1, device_id=rank(i + 1), device_id_type=MESH))
@@ -71,13 +95,20 @@
     groups = (g, across, after, before)
 
     modes[...] = jnp.zeros_like(modes)
+    fcat[:, down + EDGE + 3 * part:, :] = jnp.zeros(
+        (crs_size, LANES - (down + EDGE + 3 * part), fcat.shape[2]), jnp.float32)
+    for load in loads[:4]:
+        load.wait()
     fc = face[...]
     first_sub = me * subs
-    names = nlist[pl.ds(first_sub, subs), :]
+    line = lax.broadcasted_iota(jnp.int32, (subs, width), 0)
     target = jnp.zeros((subs, width), jnp.int32)
     for f in range(nface):
-        target = jnp.where(fc == f, names[:, f:f + 1], target)
-    third = c * subs + lax.broadcasted_iota(jnp.int32, (subs, width), 0)
+        name = jnp.zeros((subs, width), jnp.int32)
+        for s in range(subs):
+            name = jnp.where(line == s, nlist[f, first_sub + s], name)
+        target = jnp.where(fc == f, name, target)
+    third = c * subs + line
     nxt = jnp.where(third == group - 1, 0, third + 1)
     prv = jnp.where(third == 0, group - 1, third - 1)
 
@@ -102,12 +133,15 @@
             value = nbr_s * masks[d][s:s + 1, :]
             spot = pl.ds(rows[d], nk)
             modes[spot, cols] = value
-    sums = jnp.zeros((nrhs, modes.shape[0]), jnp.float32)
+    pair[...] = both(modes[...])
+    loads[4].wait()
+    sums = jnp.zeros((2 * nrhs, 2 * LANES), jnp.float32)
     for s in range(subs):
         cols = pl.ds(s * width, width)
-        sums = sums + dot3(split(mult[:, s, :]), split(modes[:, cols]), NT)
-    c_send[:, :modes.shape[0]] = sums
-    c_recv[0, c, :, :modes.shape[0]] = sums
+        sums = sums + dot(both(mult[:, s, :]), pair[:, cols], NT)
+    sums = quarters(sums)
+    c_send[...] = sums
+    c_recv[0, c] = sums
 
     pl.semaphore_wait(barrier, devices - 1)
 
@@ -165,6 +199,63 @@
             send_sem=f_ssem.at[i, n], recv_sem=f_rsem.at[i, n],
             device_id=(where, to), device_id_type=MESH).wait_recv()
 
+    loads[5].wait()
+    span = LANES // part
+    blocks = fown.shape[0]
+    for b in range(blocks):
+        held = factor[b * span * part:min((b + 1) * span, crs_size) * part, :]
+        if held.shape[0] < LANES:
+            held = jnp.concatenate(
+                [held, jnp.zeros((LANES - held.shape[0], held.shape[1]), jnp.float32)], axis=0)
+        fown[b] = both(held)
+
+    for j in (0, 1, 2, 3):
+        for i in range(crs_size):
+            if j or i:
+                c_wait(j, i)
+
+    lane = lax.broadcasted_iota(jnp.int32, (nrhs, LANES), 1)
+
+    def rolled(value, by):
+        return pltpu.roll(value, (LANES - by) % LANES, 1) if by % LANES else value
+
+    total = jnp.zeros((nrhs, factor.shape[1]), jnp.float32)
+    for b in range(blocks):
+        group_rhs = jnp.zeros((nrhs, LANES), jnp.float32)
+        for p in range(b * span, min((b + 1) * span, crs_size)):
+            at = (p - b * span) * part
+            low = c_recv[0, (p - 1) % crs_size]
+            high = c_recv[0, (p + 1) % crs_size]
+            rhs = rolled(c_recv[0, p], -at)
+            rhs = rhs + jnp.where(lane < at + EDGE, rolled(low, up - at), 0.0)
+            rhs = rhs + jnp.where(
+                lane >= at + part - EDGE, rolled(high, down - (at + part - EDGE)), 0.0)
+            rhs = rhs + rolled(c_recv[1, p], off_x - at)
+            rhs = rhs + rolled(c_recv[2, p], off_n - at)
+            rhs = rhs + rolled(c_recv[3, p], off_p - at)
+            group_rhs = jnp.where((lane >= at) & (lane < at + part), rhs, group_rhs)
+        total = total + twice(group_rhs, fown[b])
+
+    chunk = factor.shape[1] // parts
+    for q in range(parts):
+        for r in range(nrhs):
+            rs_send[q * nrhs + r] = total[r:r + 1, q * chunk:(q + 1) * chunk]
+
+    def rs_copy(i):
+        to = lax.rem(g + i, sub_size)
+        return pltpu.make_async_remote_copy(
+            src_ref=rs_send.at[to], dst_ref=rs_recv.at[g],
+            send_sem=rs_ssem.at[i], recv_sem=rs_rsem.at[i],
+            device_id=(to, c), device_id_type=MESH)
+
+    def rs_wait(i):
+        src = lax.rem(g + sub_size - i, sub_size)
+        pltpu.make_async_remote_copy(
+            src_ref=rs_send.at[src], dst_ref=rs_recv.at[src],
+            send_sem=rs_ssem.at[i], recv_sem=rs_rsem.at[i],
+            device_id=(src, c), device_id_type=MESH).wait_recv()
+
+    each(sub_size - 1, lambda i: rs_copy(i + 1).start())
     moves = [(i, n) for i in range(crs_size) for n in range(6) if i or n > 2]
     for i, n in moves:
         f_copy(i, n).start()
@@ -172,49 +263,6 @@
     for start, place, size, _ in pieces[:3]:
         fcat[c, pl.ds(place, size), :] = factor[pl.ds(start, size), :]
 
-    for j in (0, 1, 2, 3):
-        for i in range(crs_size):
-            if j or i:
-                c_wait(j, i)
-
-    lane = lax.broadcasted_iota(jnp.int32, (nrhs, LANES), 1)
-
-    def rolled(value, by):
-        return pltpu.roll(value, LANES - by, 1)
-
-    total = jnp.zeros((nrhs, factor.shape[1]), jnp.float32)
-    for p in range(crs_size):
-        low = c_recv[0, (p - 1) % crs_size]
-        high = c_recv[0, (p + 1) % crs_size]
-        rhs = c_recv[0, p]
-        rhs = rhs + jnp.where(lane < EDGE, rolled(low, up), 0.0)
-        rhs = rhs + jnp.where(lane >= part - EDGE, rolled(high, down - (part - EDGE)), 0.0)
-        rhs = rhs + rolled(c_recv[1, p], off_x)
-        rhs = rhs + rolled(c_recv[2, p], off_n)
-        rhs = rhs + rolled(c_recv[3, p], off_p)
-        total = total + dot3(
-            split(rhs[:, :part]), split(factor[p * part:(p + 1) * part, :]), NN)
-
-    chunk = factor.shape[1] // parts
-    for q in range(parts):
-        for r in range(nrhs):
-            rs_send[q * nrhs + r] = total[r:r + 1, q * chunk:(q + 1) * chunk]
-
-    def rs_copy(i):
-        to = lax.rem(g + i, sub_size)
-        return pltpu.make_async_remote_copy(
-            src_ref=rs_send.at[to], dst_ref=rs_recv.at[g],
-            send_sem=rs_ssem.at[i], recv_sem=rs_rsem.at[i],
-            device_id=(to, c), device_id_type=MESH)
-
-    def rs_wait(i):
-        src = lax.rem(g + sub_size - i, sub_size)
-        pltpu.make_async_remote_copy(
-            src_ref=rs_send.at[src], dst_ref=rs_recv.at[src],
-            send_sem=rs_ssem.at[i], recv_sem=rs_rsem.at[i],
-            device_id=(src, c), device_id_type=MESH).wait_recv()
-
-    each(sub_size - 1, lambda i: rs_copy(i + 1).start())
     rs_recv[g] = rs_send[g]
     each(sub_size - 1, lambda i: rs_wait(i + 1))
     mine = rs_recv[0]
@@ -239,18 +287,20 @@
     panel[c, g] = mine
     for i, n in moves:
         f_wait(i, n)
+    for p in range(crs_size):
+        fpair[p] = both(fcat[p])
     each(devices - 1, lambda i: ag_wait(i + 1))
 
-    amps = jnp.zeros((nrhs, modes.shape[0]), jnp.float32)
+    amps = jnp.zeros((2 * nrhs, 2 * LANES), jnp.float32)
     for p in range(crs_size):
         for q in range(parts):
             rows = panel[p, q * nrhs:(q + 1) * nrhs].reshape(nrhs, chunk)
-            amps = amps + dot3(
-                split(rows), split(fcat[p, :, q * chunk:(q + 1) * chunk]), NT)
-    amps = split(amps)
+            amps = amps + dot(both(rows), fpair[p, :, q * chunk:(q + 1) * chunk], NT)
+    amps = quarters(amps)
     for s in range(subs):
-        cols = pl.ds(s * width, width)
-        out[:, s, :] = mult[:, s, :] - dot3(amps, split(modes[:, cols]), NN)
+        out[:, s, :] = mult[:, s, :] - twice(amps, pair[:, s * width:(s + 1) * width])
+    store = pltpu.make_async_copy(out, out_h, in_sem.at[0])
+    store.start()
 
     for j in range(4):
         for i in range(crs_size):
@@ -261,27 +311,37 @@
     each(sub_size - 1, lambda i: rs_copy(i + 1).wait_send())
     each(devices - 1, lambda i: ag_copy(i + 1).wait_send())
 
+    store.wait()
+
 
 def body(sub_size, crs_size, mult, own, nbr, face, nlist, factor):
     nk, subs, width = own.shape
     nrhs = mult.shape[0]
     part = nk * subs
-    frame = 4 * part + 2 * EDGE
+    blocks = -(-crs_size // (LANES // part))
     cols = factor.shape[1]
     chunk = cols * nrhs // sub_size
     f32 = jnp.float32
     dma = pltpu.SemaphoreType.DMA
-    vmem = pl.BlockSpec(memory_space=pltpu.VMEM)
+    bf16 = jnp.bfloat16
+    hbm = pl.BlockSpec(memory_space=pl.ANY)
+    names = nlist.T
     return pl.pallas_call(
         functools.partial(kernel, sub_size, crs_size),
         out_shape=jax.ShapeDtypeStruct(mult.shape, mult.dtype),
-        in_specs=[vmem] * 6,
-        out_specs=vmem,
+        in_specs=[hbm] * 6,
+        out_specs=hbm,
         scratch_shapes=[
-            pltpu.VMEM((frame, subs * width), f32),
+            pltpu.VMEM(mult.shape, f32), pltpu.VMEM(own.shape, f32), pltpu.VMEM(nbr.shape, f32),
+            pltpu.VMEM(face.shape, face.dtype), pltpu.SMEM(names.shape, names.dtype),
+            pltpu.VMEM(factor.shape, f32), pltpu.VMEM(mult.shape, f32),
+            pltpu.VMEM((LANES, subs * width), f32),
+            pltpu.VMEM((2 * LANES, subs * width), bf16),
             pltpu.VMEM((nrhs, LANES), f32),
             pltpu.VMEM((4, crs_size, nrhs, LANES), f32),
-            pltpu.VMEM((crs_size, frame, cols), f32),
+            pltpu.VMEM((crs_size, LANES, cols), f32),
+            pltpu.VMEM((blocks, 2 * LANES, cols), bf16),
+            pltpu.VMEM((crs_size, 2 * LANES, cols), bf16),
             pltpu.VMEM((sub_size, 1, chunk), f32),
             pltpu.VMEM((sub_size, 1, chunk), f32),
             pltpu.VMEM((1, chunk), f32),
@@ -289,10 +349,10 @@
             dma((4, crs_size)), dma((4, crs_size)),
             dma((crs_size, 6)), dma((crs_size, 6)),
             dma((sub_size,)), dma((sub_size,)),
-            dma((sub_size * crs_size,)), dma((sub_size * crs_size,)),
+            dma((sub_size * crs_size,)), dma((sub_size * crs_size,)), dma((6,)),
         ],
         compiler_params=pltpu.CompilerParams(collective_id=0, has_side_effects=True),
-    )(mult, own, nbr, face, nlist, factor)
+    )(mult, own, nbr, face, names, factor)
 
 
 def solution(mesh):

time: 26.5 us -> 23.3 us (0.88)
  Pallas kernels: 23.3 us -> 21.6 us
  local copies, waits for them, and re-layouts: 2.99 us -> 1.57 us
    pallas_call x1, Pallas kernels: 23.3 us -> 21.6 us  [body(): pl.pallas_call(functools.partial(kernel, sub_size, crs_size), out_shape=j...]
    unnamed x2 -> x1, local copies, waits for them, and re-layouts: 2.99 us -> 1.57 us
where the time goes in v2:
time: 23.3 us; the launch traced here: 23.2 us
  Pallas kernels  21.6 us (93%)
  local copies, waits for them, and re-layouts  1.57 us (7%)
    pallas_call x1, Pallas kernels, body(): pl.pallas_call(functools.partial(kernel, sub_size, crs_size), out_shape=j...  21.6 us
    unnamed x1, local copies, waits for them, and re-layouts  1.57 us

profile of v2, /device:TPU:0, one launch (start us, length us, event | category | flops | bytes accessed | tf_op | source)
XLA Modules:
  0.0 23.2 jit_solution(4641271807165654291)
XLA Ops:
  0.0 21.6 %shard_map.64 = f32[16,4,512]{2,1,0:T(4,128)} custom-call(f32[16,4,512]{2,1,0:T(4,128)} %mult_h.1, f32[6,4,512]{2,1,0:T(4,128)} %own_h.1, f32[6,4,512]{2,1,0:T(4,128)} %nbr_h.1, s32[4,512]{1,0:T(4,128)} %face_h.1, s32[6,128]{1,0:T(8,128)} %bitcast.1, f32[48,384]{1,0:T(8,128)} %factor_h.1), custom_call_target="tpu_custom_call" | custom-call | tf_op jit(solution)/shard_map/pallas_call | solution.py:329
  21.6 1.6 %copy.8 = f32[16,4,512]{2,1,0:T(4,128)} copy(f32[16,4,512]{2,1,0:T(4,128)} %shard_map.64) | data formatting | bytes 262144

commit v3 on v2

--- a/solution.py
+++ b/solution.py
@@ -56,7 +56,7 @@
     mult_h, own_h, nbr_h, face_h, nlist_h, factor_h, out_h,
     mult, own, nbr, face, nlist, factor, out,
     modes, pair, c_send, c_recv, fcat, fown, fpair, rs_send, rs_recv, ag_send, panel,
-    c_ssem, c_rsem, f_ssem, f_rsem, rs_ssem, rs_rsem, ag_ssem, ag_rsem, in_sem,
+    c_ssem, c_rsem, f_ssem, f_rsem, rs_ssem, rs_rsem, ag_ssem, ag_rsem, in_sem, met,
 ):
     nk, subs, width = own.shape
     nrhs = mult.shape[0]
@@ -85,14 +85,26 @@
     for load in loads:
         load.start()
     barrier = pltpu.get_barrier_semaphore()
-    each(devices - 1, lambda i: pl.semaphore_signal(
-        barrier, inc=1, device_id=rank(i + 1), device_id_type=MESH))
-
     first, second = g // row_len, lax.rem(g, row_len)
     across = lax.rem(first + 1, 2) * row_len + second
     after = first * row_len + lax.rem(second + 1, row_len)
     before = first * row_len + lax.rem(second + row_len - 1, row_len)
     groups = (g, across, after, before)
+
+    block = 1 << (devices.bit_length() // 2)
+    base = me // block * block
+    inner = [base + lax.rem(me - base + i, block) for i in range(1, block)]
+    outer = [lax.rem(me + i, devices) for i in range(block, devices, block)]
+    near = [groups[j] * crs_size + lax.rem(c + i, crs_size)
+            for j in range(4) for i in range(crs_size) if j or i]
+
+    def signal(semaphore, other):
+        pl.semaphore_signal(
+            semaphore, inc=1, device_id=(other // crs_size, lax.rem(other, crs_size)),
+            device_id_type=MESH)
+
+    for other in outer + near + inner:
+        signal(barrier, other)
 
     modes[...] = jnp.zeros_like(modes)
     fcat[:, down + EDGE + 3 * part:, :] = jnp.zeros(
@@ -143,7 +155,7 @@
     c_send[...] = sums
     c_recv[0, c] = sums
 
-    pl.semaphore_wait(barrier, devices - 1)
+    pl.semaphore_wait(barrier, len(outer) + len(near) + len(inner))
 
     def c_copy(j, i):
         to = lax.rem(c + i, crs_size)
@@ -198,6 +210,9 @@
             dst_ref=fcat.at[src, pl.ds(place, size), :],
             send_sem=f_ssem.at[i, n], recv_sem=f_rsem.at[i, n],
             device_id=(where, to), device_id_type=MESH).wait_recv()
+
+    for other in outer:
+        signal(met, other)
 
     loads[5].wait()
     span = LANES // part
@@ -255,6 +270,7 @@
             send_sem=rs_ssem.at[i], recv_sem=rs_rsem.at[i],
             device_id=(src, c), device_id_type=MESH).wait_recv()
 
+    pl.semaphore_wait(met, len(outer))
     each(sub_size - 1, lambda i: rs_copy(i + 1).start())
     moves = [(i, n) for i in range(crs_size) for n in range(6) if i or n > 2]
     for i, n in moves:
@@ -350,6 +366,7 @@
             dma((crs_size, 6)), dma((crs_size, 6)),
             dma((sub_size,)), dma((sub_size,)),
             dma((sub_size * crs_size,)), dma((sub_size * crs_size,)), dma((6,)),
+            pltpu.SemaphoreType.REGULAR,
         ],
         compiler_params=pltpu.CompilerParams(collective_id=0, has_side_effects=True),
     )(mult, own, nbr, face, names, factor)

time: 23.3 us -> 23.4 us (level)
  no operation moved by 1% of the time
where the time goes in v3:
time: 23.4 us; the launch traced here: 23.2 us
  Pallas kernels  21.6 us (92%)
  local copies, waits for them, and re-layouts  1.57 us (7%)
    pallas_call x1, Pallas kernels, body(): pl.pallas_call(functools.partial(kernel, sub_size, crs_size), out_shape=j...  21.6 us
    unnamed x1, local copies, waits for them, and re-layouts  1.57 us

profile of v3, /device:TPU:0, one launch (start us, length us, event | category | flops | bytes accessed | tf_op | source)
XLA Modules:
  0.0 23.2 jit_solution(3585588341593563089)
XLA Ops:
  0.0 21.6 %shard_map.64 = f32[16,4,512]{2,1,0:T(4,128)} custom-call(f32[16,4,512]{2,1,0:T(4,128)} %mult_h.1, f32[6,4,512]{2,1,0:T(4,128)} %own_h.1, f32[6,4,512]{2,1,0:T(4,128)} %nbr_h.1, s32[4,512]{1,0:T(4,128)} %face_h.1, s32[6,128]{1,0:T(8,128)} %bitcast.1, f32[48,384]{1,0:T(8,128)} %factor_h.1), custom_call_target="tpu_custom_call" | custom-call | tf_op jit(solution)/shard_map/pallas_call | solution.py:345
  21.6 1.6 %copy.8 = f32[16,4,512]{2,1,0:T(4,128)} copy(f32[16,4,512]{2,1,0:T(4,128)} %shard_map.64) | data formatting | bytes 262144

commit v4 on v3

--- a/solution.py
+++ b/solution.py
@@ -16,7 +16,7 @@
 
 def each(count, step):
     if count <= 64:
-        for i in range(count):
+        for i in sorted(range(count), key=lambda i: min(i, count - 1 - i)):
             step(i)
     else:
         lax.fori_loop(0, count, lambda i, t: (step(i), t)[1], 0)
@@ -54,7 +54,7 @@
 def kernel(
     sub_size, crs_size,
     mult_h, own_h, nbr_h, face_h, nlist_h, factor_h, out_h,
-    mult, own, nbr, face, nlist, factor, out,
+    mult, own, nbr, face, nlist, factor,
     modes, pair, c_send, c_recv, fcat, fown, fpair, rs_send, rs_recv, ag_send, panel,
     c_ssem, c_rsem, f_ssem, f_rsem, rs_ssem, rs_rsem, ag_ssem, ag_rsem, in_sem, met,
 ):
@@ -314,9 +314,7 @@
             amps = amps + dot(both(rows), fpair[p, :, q * chunk:(q + 1) * chunk], NT)
     amps = quarters(amps)
     for s in range(subs):
-        out[:, s, :] = mult[:, s, :] - twice(amps, pair[:, s * width:(s + 1) * width])
-    store = pltpu.make_async_copy(out, out_h, in_sem.at[0])
-    store.start()
+        out_h[:, s, :] = twice(amps, pair[:, s * width:(s + 1) * width])
 
     for j in range(4):
         for i in range(crs_size):
@@ -326,8 +324,6 @@
         f_copy(i, n).wait_send()
     each(sub_size - 1, lambda i: rs_copy(i + 1).wait_send())
     each(devices - 1, lambda i: ag_copy(i + 1).wait_send())
-
-    store.wait()
 
 
 def body(sub_size, crs_size, mult, own, nbr, face, nlist, factor):
@@ -342,15 +338,15 @@
     bf16 = jnp.bfloat16
     hbm = pl.BlockSpec(memory_space=pl.ANY)
     names = nlist.T
-    return pl.pallas_call(
+    applied = pl.pallas_call(
         functools.partial(kernel, sub_size, crs_size),
-        out_shape=jax.ShapeDtypeStruct(mult.shape, mult.dtype),
+        out_shape=pltpu.VMEM(mult.shape, mult.dtype),
         in_specs=[hbm] * 6,
-        out_specs=hbm,
+        out_specs=pl.BlockSpec(memory_space=pltpu.VMEM),
         scratch_shapes=[
             pltpu.VMEM(mult.shape, f32), pltpu.VMEM(own.shape, f32), pltpu.VMEM(nbr.shape, f32),
             pltpu.VMEM(face.shape, face.dtype), pltpu.SMEM(names.shape, names.dtype),
-            pltpu.VMEM(factor.shape, f32), pltpu.VMEM(mult.shape, f32),
+            pltpu.VMEM(factor.shape, f32),
             pltpu.VMEM((LANES, subs * width), f32),
             pltpu.VMEM((2 * LANES, subs * width), bf16),
             pltpu.VMEM((nrhs, LANES), f32),
@@ -370,6 +366,7 @@
         ],
         compiler_params=pltpu.CompilerParams(collective_id=0, has_side_effects=True),
     )(mult, own, nbr, face, names, factor)
+    return mult - applied
 
 
 def solution(mesh):

time: 23.4 us -> 21.7 us (0.927)
  local copies, waits for them, and re-layouts: 1.57 us -> 0.01 us
  Pallas kernels: 21.6 us -> 20.9 us
  other arithmetic: 0 us -> 0.69 us
    unnamed x1 -> x2, local copies, waits for them, and re-layouts: 1.57 us -> 0.01 us
    pallas_call x1, Pallas kernels: 21.6 us -> 20.9 us  [body(): pl.pallas_call(functools.partial(kernel, sub_size, crs_size), out_shape=p...]
    sub x0 -> x1, other arithmetic: none -> 0.69 us  [body(): return mult - applied]
where the time goes in v4:
time: 21.7 us; the launch traced here: 21.6 us
  Pallas kernels  20.9 us (96%)
  other arithmetic  0.69 us (3%)
    pallas_call x1, Pallas kernels, body(): pl.pallas_call(functools.partial(kernel, sub_size, crs_size), out_shape=p...  20.9 us
    sub x1, other arithmetic, body(): return mult - applied  0.69 us

profile of v4, /device:TPU:0, one launch (start us, length us, event | category | flops | bytes accessed | tf_op | source)
XLA Modules:
  0.0 21.6 jit_solution(11431670355576670208)
XLA Ops:
  0.0 0.0 copy-start
  0.0 20.9 %shard_map.64 = f32[16,4,512]{2,1,0:T(4,128)S(1)} custom-call(f32[16,4,512]{2,1,0:T(4,128)} %mult_h.1, f32[6,4,512]{2,1,0:T(4,128)} %own_h.1, f32[6,4,512]{2,1,0:T(4,128)} %nbr_h.1, s32[4,512]{1,0:T(4,128)} %face_h.1, s32[6,128]{1,0:T(8,128)} %bitcast.1, f32[48,384]{1,0:T(8,128)} %factor_h.1), custom_call_target="tpu_custom_call" | custom-call | tf_op jit(solution)/shard_map/pallas_call | solution.py:341
  20.9 0.0 copy-done
  20.9 0.7 %sub.3 = f32[16,4,512]{2,1,0:T(4,128)} subtract(f32[16,4,512]{2,1,0:T(4,128)S(1)} %copy-done, f32[16,4,512]{2,1,0:T(4,128)S(1)} %shard_map.64) | non-fusion elementwise | flops 32768 | bytes 393216 | tf_op jit(solution)/shard_map/sub | solution.py:369
Async XLA Ops:
  0.0 20.9 %copy-start = (f32[16,4,512]{2,1,0:T(4,128)S(1)}, f32[16,4,512]{2,1,0:T(4,128)}, u32[]{:S(2)}) copy-start(f32[16,4,512]{2,1,0:T(4,128)} %mult_h.1) | copy-start | bytes 393220
